TPU v7x, 32 devices: a whole 2x2x4 slice. The times are simulated.
32 devices in a mesh: grp: 4 (over y, x), grid: 8 (over z, core).
Axes of the slice: x: 2, y: 2, z: 4, core: 2. Of those that a mesh axis runs over, the one named last changes fastest.
Arguments:
- orbitals: float32 [64, 262144], P('grp', 'grid'), may hold values from -6 to 6
- anchors: int32 [64, 3], replicated, may hold values from 0 to 31
- pair_slots: int32 [32, 4, 2], replicated, may hold values from -1 to 63, as said below
Outputs:
- exchange_term: float32 [64, 262144], P('grp', 'grid')
Inputs may be any that keep to these rules, and one draw needn't show every extreme that they name: `pair_slots`: row k lists the pairs of owner k, the device with index k in the order grp, grid; its first slots hold pairs of two different orbital numbers and its other slots hold -1 in both columns. Exactly 64 slots hold pairs in all, no row holds more than 4, and some row holds exactly 4.
All inputs are finite; a program needn't handle non-finite values.
Results may differ from a plain program's by a relative error of at most 0.0003.
Values sent between devices are 32-bit elements; how exact they have to be, the bound alone decides.
A program may use at most 128 MiB of HBM per device.

v0:
```python
import jax
import jax.numpy as jnp
from jax import lax
from jax.sharding import PartitionSpec as P

B = 64
PAIR_DEV = 2
ITERS = 3


def shift_field(field, offset, extent):
    plane_size = extent * extent
    padded_x = jnp.pad(field, ((extent, extent), (0, 0)))
    moved = lax.dynamic_slice_in_dim(padded_x, extent - offset[0], extent, 0)
    padded_yz = jnp.pad(moved, ((0, 0), (plane_size, plane_size)))
    linear = offset[1] * extent + offset[2]
    moved = lax.dynamic_slice_in_dim(padded_yz, plane_size - linear, plane_size, 1)
    cells = lax.broadcasted_iota(jnp.int32, (1, plane_size), 1)
    coord_y = cells // extent - offset[1]
    coord_z = cells % extent - offset[2]
    inside = (coord_y >= 0) & (coord_y < extent) & (coord_z >= 0) & (coord_z < extent)
    return jnp.where(inside, moved, jnp.zeros_like(moved))


def operate(field, extent):
    padded_x = jnp.pad(field, ((1, 1), (0, 0)))
    beside = padded_x[2:] + padded_x[:-2]
    padded_y = jnp.pad(field, ((0, 0), (extent, extent)))
    beside = beside + padded_y[:, 2 * extent :] + padded_y[:, : -2 * extent]
    padded_z = jnp.pad(field, ((0, 0), (1, 1)))
    cells = lax.broadcasted_iota(jnp.int32, (1, field.shape[1]), 1) % extent
    upper_z = jnp.where(cells < extent - 1, padded_z[:, 2:], jnp.zeros_like(field))
    lower_z = jnp.where(cells > 0, padded_z[:, :-2], jnp.zeros_like(field))
    return 6.0 * field - beside - upper_z - lower_z


def conjugate(density, extent):
    potential = jnp.zeros_like(density)
    resid = density
    direction = density
    norm_now = jnp.sum(resid * resid)
    for turn in range(ITERS):
        image = operate(direction, extent)
        step_len = norm_now / jnp.sum(direction * image)
        potential = potential + step_len * direction
        resid = resid - step_len * image
        norm_next = jnp.sum(resid * resid)
        direction = resid + norm_next / norm_now * direction
        norm_now = norm_next
    return potential


def pair_terms(field_a, field_b, offset, extent):
    partner = shift_field(field_b, offset, extent)
    density = field_a * partner
    potential = conjugate(density, extent)
    term_a = potential * partner
    term_b = shift_field(potential * field_a, -offset, extent)
    return (term_a, term_b)


def deal_evenly(pair_slots, owner_count, each_owner):
    flat_slots = pair_slots.reshape(-1, 2)
    filled = (flat_slots[:, 0] >= 0).astype(jnp.int32)
    position = jnp.cumsum(filled, dtype=jnp.int32) - filled
    wanted = lax.broadcasted_iota(jnp.int32, (owner_count, each_owner), 1) * owner_count
    wanted = (wanted + lax.broadcasted_iota(jnp.int32, (owner_count, each_owner), 0)).reshape(-1)
    matched = (position[None, :] == wanted[:, None]) & (filled[None, :] == 1)
    picked = jnp.dot(matched.astype(jnp.int32), flat_slots)
    return picked.reshape(owner_count, each_owner, 2)


def body(orbitals, anchors, pair_slots):
    extent = B
    grid_count = lax.axis_size("grid")
    owner_count = lax.axis_size("grp") * grid_count
    group_idx = lax.axis_index("grp")
    place_idx = lax.axis_index("grid")
    assignment = deal_evenly(pair_slots, owner_count, PAIR_DEV)
    slot_count = assignment.shape[1]
    filled = assignment[..., 0] >= 0
    safe_ids = jnp.maximum(assignment, 0)
    pieces = lax.all_gather(orbitals, "grp", axis=0, tiled=True)
    group_table = lax.dynamic_slice_in_dim(safe_ids, group_idx * grid_count, grid_count, 0)
    gather_ids = jnp.transpose(group_table, (1, 2, 0))
    outgoing = pieces[gather_ids]
    arrived = lax.all_to_all(outgoing, "grid", split_axis=2, concat_axis=2, tiled=True)
    boxes = arrived.reshape(slot_count, 2, extent, extent * extent)
    owner_idx = group_idx * grid_count + place_idx
    own_pairs = safe_ids[owner_idx]
    own_filled = filled[owner_idx]
    offsets = anchors[own_pairs[:, 1]] - anchors[own_pairs[:, 0]]

    def solve_slot(slot_item):
        boxes_pair, offset, flag = slot_item
        term_a, term_b = pair_terms(boxes_pair[0], boxes_pair[1], offset, extent)
        weight_flag = jnp.where(flag, 1.0, 0.0).astype(jnp.float32)
        return jnp.stack([term_a, term_b]) * weight_flag

    terms = lax.map(solve_slot, (boxes, offsets, own_filled))
    returned = lax.all_to_all(
        terms.reshape(slot_count, 2, grid_count, -1),
        "grid",
        split_axis=2,
        concat_axis=2,
        tiled=True,
    )
    flat_terms = returned.reshape(-1, returned.shape[-1])
    summed = jax.ops.segment_sum(flat_terms, gather_ids.reshape(-1), num_segments=anchors.shape[0])
    return lax.psum_scatter(summed, "grp", scatter_dimension=0, tiled=True)


def solution(mesh):
    return jax.shard_map(
        body,
        mesh=mesh,
        in_specs=(P("grp", "grid"), P(), P()),
        out_specs=P("grp", "grid"),
        check_vma=False,
    )
```

profile of v0, /device:TPU:0, one launch (start us, length us, event | category | flops | bytes accessed | tf_op | source)
XLA Modules:
  0.0 509.3 jit_solution(14262574383303529083)
XLA Ops:
  9.0 90.4 %all-gather.2.cloned.1.call-done = f32[64,32768]{1,0:T(8,128)} async-done(((f32[16,32768]{1,0:T(8,128)}), f32[64,32768]{1,0:T(8,128)}) %all-gather.2.cloned.1.call-update) | async-done | bytes 8388624 | tf_op jit(solution)/shard_map/all_gather | solution.py:83
  99.4 8.8 %gather_fusion = f32[32,32768]{1,0:T(8,128)} fusion(f32[64,32768]{1,0:T(8,128)} %all-gather.2.cloned.1.call-done, s32[1024]{0:T(1024)S(1)} %pad_clamp_fusion.2), kind=kCustom, calls=%fused_computation | custom fusion | bytes 8388736 | tf_op jit(solution)/shard_map/gather | solution.py:86
  108.2 7.4 %copy.19 = f32[2,2,8,32768]{3,1,0,2:T(2,128)} copy(f32[2,2,8,32768]{3,2,1,0:T(8,128)} %bitcast.60) | data formatting | bytes 8388608 | tf_op jit(solution)/shard_map/gather | solution.py:86
  115.6 4.9 all-to-all-start
  122.3 92.1 %all-to-all-done = f32[2,2,8,32768]{3,1,0,2:T(2,128)} async-done(((f32[2,2,8,32768]{3,1,0,2:T(2,128)}), f32[2,2,8,32768]{3,1,0,2:T(2,128)}, u32[]{:S(2)}, u32[]{:S(2)}) %all-to-all-start) | async-done | bytes 4194336 | tf_op jit(solution)/shard_map/all_to_all | solution.py:87
  214.4 6.6 %copy.20 = f32[2,2,8,32768]{3,2,1,0:T(8,128)} copy(f32[2,2,8,32768]{3,1,0,2:T(2,128)} %all-to-all-done) | data formatting | bytes 8388608 | tf_op jit(solution)/shard_map/all_to_all | solution.py:87
  221.0 4.9 reshape.254
  226.0 64.2 %while.13 = (s32[]{:T(128)}, f32[2,2,64,4096]{3,2,1,0:T(8,128)}, f32[2,2,64,4096]{3,2,1,0:T(8,128)}, s32[2,3]{1,0:T(2,128)S(1)}, pred[2]{0:T(512)(128)(4,1)S(1)}...) while((s32[]{:T(128)}, f32[2,2,64,4096]{3,2,1,0:T(8,128)}, ...), condition=%wide.region_8.9_spmd, body=%wide.region_1.8_spmd.sunk | while | flops 22224920 | bytes 80794384 | solution.py:100
  232.8 1.2 fusion.85
  234.0 1.2 fusion.81
  235.3 1.3 dynamic-slice_bitcast_fusion.5
  237.7 1.6 fusion.82
  239.3 1.8 multiply_reduce_fusion.9
  244.5 1.8 multiply_reduce_fusion.11
  250.0 1.8 fusion.84
  253.0 2.3 multiply_bitcast_fusion.2
  256.0 2.0 copy-done.2
  266.1 1.2 fusion.81
  267.3 1.3 dynamic-slice_bitcast_fusion.5
  269.7 1.6 fusion.82
  271.3 1.8 multiply_reduce_fusion.9
  276.6 1.8 multiply_reduce_fusion.11
  282.1 1.8 fusion.84
  285.1 2.3 multiply_bitcast_fusion.2
  288.2 2.0 copy-done.2
  290.2 4.9 reshape.255
  295.1 7.4 %copy.23 = f32[2,2,8,32768]{3,1,0,2:T(2,128)} copy(f32[2,2,8,32768]{3,2,1,0:T(8,128)} %reshape.255) | data formatting | bytes 8388608 | tf_op jit(solution)/shard_map/reshape | solution.py:102
  302.5 4.5 all-to-all-start.1
  307.2 93.8 %all-to-all-done.1 = f32[2,2,8,32768]{3,1,0,2:T(2,128)} async-done(((f32[2,2,8,32768]{3,1,0,2:T(2,128)}), f32[2,2,8,32768]{3,1,0,2:T(2,128)}, u32[]{:S(2)}, u32[]{:S(2)}) %all-to-all-start.1) | async-done | bytes 4194336 | tf_op jit(solution)/shard_map/all_to_all | solution.py:101
  401.0 6.6 %copy.24 = f32[2,2,8,32768]{3,2,1,0:T(8,128)} copy(f32[2,2,8,32768]{3,1,0,2:T(2,128)} %all-to-all-done.1) | data formatting | bytes 8388608 | tf_op jit(solution)/shard_map/all_to_all | solution.py:101
  407.6 10.4 %scatter_custom_fusion = f32[64,32768]{1,0:T(8,128)} fusion(s32[32]{0:T(128)S(1)} %reshape.283, f32[32,32768]{1,0:T(8,128)} %bitcast.61, f32[]{:T(128)} %constant.162.clone.1), kind=kCustom, calls=%fused_computation.86 | custom fusion | flops 1048576 | bytes 8389120 | tf_op jit(solution)/shard_map/scatter-add | solution.py:109
  418.0 84.4 %reduce-scatter.2.cloned.1.call-done = f32[16,32768]{1,0:T(8,128)} async-done(((f32[64,32768]{1,0:T(8,128)}), f32[16,32768]{1,0:T(8,128)}) %reduce-scatter.2.cloned.1.call-update) | async-done | bytes 2097168 | tf_op jit(solution)/shard_map/reduce_scatter | solution.py:110
  (62 shorter events, 16.1 us)
Async XLA Ops:
  6.5 92.9 %all-gather.2.cloned.1.call-start = ((), (), s32[]{:S(2)}) async-start(), calls=%async_computation.3 | async-start | bytes 10485760 | tf_op jit(solution)/shard_map/all_gather | solution.py:83
  115.6 4.9 copy-start.3
  115.6 98.8 %all-to-all-start = ((f32[2,2,8,32768]{3,1,0,2:T(2,128)}), f32[2,2,8,32768]{3,1,0,2:T(2,128)}, u32[]{:S(2)}, u32[]{:S(2)}) async-start(f32[2,2,8,32768]{3,1,0,2:T(2,128)} %copy.19), calls=%async_computation | async-start | bytes 8388608 | tf_op jit(solution)/shard_map/all_to_all | solution.py:87
  236.7 1.0 copy-start
  253.0 2.8 copy-start.1
  256.0 2.0 copy-start.2
  268.8 1.0 copy-start
  285.1 2.8 copy-start.1
  288.2 2.0 copy-start.2
  302.5 98.5 %all-to-all-start.1 = ((f32[2,2,8,32768]{3,1,0,2:T(2,128)}), f32[2,2,8,32768]{3,1,0,2:T(2,128)}, u32[]{:S(2)}, u32[]{:S(2)}) async-start(f32[2,2,8,32768]{3,1,0,2:T(2,128)} %copy.23), calls=%async_computation.1 | async-start | bytes 8388608 | tf_op jit(solution)/shard_map/all_to_all | solution.py:101
  307.0 195.4 %reduce-scatter.2.cloned.1.call-start = ((), (), s32[]{:S(2)}) async-start(), calls=%async_computation.4 | async-start | bytes 10485760 | tf_op jit(solution)/shard_map/reduce_scatter | solution.py:110
Sparse Core Ops, SparseCore 0:
  9.2 90.1 all-gather.1
  418.1 84.2 reduce-scatter.1
where the time goes:
time: 511 us; the launch traced here: 509 us
  waiting for transfers between devices  362 us (71%)
  local copies, waits for them, and re-layouts  60.4 us (12%)
  other arithmetic  40.1 us (8%)
  loops' own time  24.1 us (5%)
  between operations  13.5 us (3%)
  starting transfers between devices  9.44 us (2%)
    all_to_all x1, waiting for transfers between devices, body(): lax.all_to_all(terms.reshape(slot_count, 2, grid_count, -1), 'grid', spli...  93.8 us
    all_to_all x1, waiting for transfers between devices, body(): lax.all_to_all(outgoing, 'grid', split_axis=2, concat_axis=2, tiled=True)  92.1 us
    all_gather x1, waiting for transfers between devices, body(): pieces = lax.all_gather(orbitals, 'grp', axis=0, tiled=True)  90.4 us
    reduce_scatter x1, waiting for transfers between devices, body(): return lax.psum_scatter(summed, 'grp', scatter_dimension=0, tiled=True)  84.4 us
    another operation x1, loops' own time, body(): terms = lax.map(solve_slot, (boxes, offsets, own_filled))  24.1 us
    gather x2, local copies, waits for them, and re-layouts, body(): outgoing = pieces[gather_ids]  16.2 us
    reshape x2, local copies, waits for them, and re-layouts, body(): terms.reshape(slot_count, 2, grid_count, -1)  12.3 us
    reduce_sum x6, other arithmetic, conjugate(): step_len = norm_now / jnp.sum(direction * image)  10.6 us
  transfers between devices with their start and end apart: 4, of which 4 were waited for; matrix products, arithmetic and copies ran while one was open for 1% of the time, Pallas kernels for 0%

commit v1 on v0

--- a/solution.py
+++ b/solution.py
@@ -98,13 +98,10 @@
         return jnp.stack([term_a, term_b]) * weight_flag
 
     terms = lax.map(solve_slot, (boxes, offsets, own_filled))
-    returned = lax.all_to_all(
-        terms.reshape(slot_count, 2, grid_count, -1),
-        "grid",
-        split_axis=2,
-        concat_axis=2,
-        tiled=True,
-    )
+    vector = terms.reshape(slot_count, 2, grid_count, -1)
+    current_block = lax.axis_size("grid")
+    tmp = jnp.stack(jnp.split(vector, current_block, 2), axis=0)
+    returned = jnp.concatenate(lax.all_to_all(tmp, "grid", 0, 0), 2)
     flat_terms = returned.reshape(-1, returned.shape[-1])
     summed = jax.ops.segment_sum(flat_terms, gather_ids.reshape(-1), num_segments=anchors.shape[0])
     return lax.psum_scatter(summed, "grp", scatter_dimension=0, tiled=True)

time: 511 us -> 531 us (1.039)
  local copies, waits for them, and re-layouts: 60.4 us -> 80.4 us
    unnamed x4 -> x11, local copies, waits for them, and re-layouts: 0.89 us -> 24.8 us
    all_to_all x1 -> x0, local copies, waits for them, and re-layouts: 6.59 us -> none  [body(): lax.all_to_all(terms.reshape(slot_count, 2, grid_count, -1), 'grid', spli...]
where the time goes in v1:
time: 531 us; the launch traced here: 529 us
  waiting for transfers between devices  362 us (68%)
  local copies, waits for them, and re-layouts  80.4 us (15%)
  other arithmetic  40.3 us (8%)
  loops' own time  23.9 us (5%)
  between operations  13.5 us (3%)
  starting transfers between devices  9.45 us (2%)
    all_to_all x1, waiting for transfers between devices, body(): returned = jnp.concatenate(lax.all_to_all(tmp, 'grid', 0, 0), 2)  93.8 us
    all_to_all x1, waiting for transfers between devices, body(): lax.all_to_all(outgoing, 'grid', split_axis=2, concat_axis=2, tiled=True)  92.1 us
    all_gather x1, waiting for transfers between devices, body(): pieces = lax.all_gather(orbitals, 'grp', axis=0, tiled=True)  90.4 us
    reduce_scatter x1, waiting for transfers between devices, body(): return lax.psum_scatter(summed, 'grp', scatter_dimension=0, tiled=True)  84.4 us
    unnamed x11, local copies, waits for them, and re-layouts  24.8 us
    another operation x1, loops' own time, body(): terms = lax.map(solve_slot, (boxes, offsets, own_filled))  23.9 us
    gather x2, local copies, waits for them, and re-layouts, body(): outgoing = pieces[gather_ids]  16.2 us
  transfers between devices with their start and end apart: 4, of which 4 were waited for; matrix products, arithmetic and copies ran while one was open for 1% of the time, Pallas kernels for 0%

profile of v1, /device:TPU:0, one launch (start us, length us, event | category | flops | bytes accessed | tf_op | source)
XLA Modules:
  0.0 529.2 jit_solution(410441295305555252)
XLA Ops:
  9.0 90.4 %all-gather.2.cloned.1.call-done = f32[64,32768]{1,0:T(8,128)} async-done(((f32[16,32768]{1,0:T(8,128)}), f32[64,32768]{1,0:T(8,128)}) %all-gather.2.cloned.1.call-update) | async-done | bytes 8388624 | tf_op jit(solution)/shard_map/all_gather | solution.py:83
  99.4 8.8 %gather_fusion = f32[32,32768]{1,0:T(8,128)} fusion(f32[64,32768]{1,0:T(8,128)} %all-gather.2.cloned.1.call-done, s32[1024]{0:T(1024)S(1)} %pad_clamp_fusion.2), kind=kCustom, calls=%fused_computation | custom fusion | bytes 8388736 | tf_op jit(solution)/shard_map/gather | solution.py:86
  108.2 7.4 %copy.28 = f32[2,2,8,32768]{3,1,0,2:T(2,128)} copy(f32[2,2,8,32768]{3,2,1,0:T(8,128)} %bitcast.93) | data formatting | bytes 8388608 | tf_op jit(solution)/shard_map/gather | solution.py:86
  115.6 4.9 all-to-all-start
  122.3 92.1 %all-to-all-done = f32[2,2,8,32768]{3,1,0,2:T(2,128)} async-done(((f32[2,2,8,32768]{3,1,0,2:T(2,128)}), f32[2,2,8,32768]{3,1,0,2:T(2,128)}, u32[]{:S(2)}, u32[]{:S(2)}) %all-to-all-start) | async-done | bytes 4194336 | tf_op jit(solution)/shard_map/all_to_all | solution.py:87
  214.4 6.6 %copy.29 = f32[2,2,8,32768]{3,2,1,0:T(8,128)} copy(f32[2,2,8,32768]{3,1,0,2:T(2,128)} %all-to-all-done) | data formatting | bytes 8388608 | tf_op jit(solution)/shard_map/all_to_all | solution.py:87
  221.0 5.0 reshape.254
  225.9 64.2 %while.13 = (s32[]{:T(128)}, f32[2,2,64,4096]{3,2,1,0:T(8,128)}, f32[2,2,64,4096]{3,2,1,0:T(8,128)}, s32[2,3]{1,0:T(2,128)S(1)}, pred[2]{0:T(512)(128)(4,1)S(1)}...) while((s32[]{:T(128)}, f32[2,2,64,4096]{3,2,1,0:T(8,128)}, ...), condition=%wide.region_8.9_spmd, body=%wide.region_1.8_spmd.sunk | while | flops 22224920 | bytes 80794384 | solution.py:100
  239.3 1.8 multiply_reduce_fusion.9
  244.6 1.8 multiply_reduce_fusion.11
  250.0 1.8 fusion.92
  253.0 2.3 multiply_bitcast_fusion.2
  256.1 1.9 copy-done.2
  271.4 1.8 multiply_reduce_fusion.9
  276.6 1.8 multiply_reduce_fusion.11
  282.1 1.8 fusion.92
  285.1 2.3 multiply_bitcast_fusion.2
  288.2 1.9 copy-done.2
  290.1 5.0 reshape.255
  295.1 3.2 fusion.62
  298.3 3.4 fusion.61
  301.8 3.5 fusion.60
  305.2 3.4 fusion.59
  308.7 3.4 fusion.58
  312.1 3.4 fusion.57
  315.6 3.4 fusion.56
  319.0 3.4 fusion.55
  322.4 4.5 all-to-all-start.1
  327.1 93.8 %all-to-all-done.1 = f32[8,2,2,1,32768]{4,3,2,1,0:T(1,128)} async-done(((f32[8,2,2,1,32768]{4,3,2,1,0:T(1,128)}), f32[8,2,2,1,32768]{4,3,2,1,0:T(1,128)}, u32[]{:S(2)}, u32[]{:S(2)}) %all-to-all-start.1) | async-done | bytes 4194336 | tf_op jit(solution)/shard_map/all_to_all | solution.py:104
  421.0 6.5 %copy.32 = f32[2,2,8,1,32768]{4,2,1,0,3:T(8,128)} copy(f32[2,2,8,1,32768]{4,3,1,0,2:T(1,128)} %bitcast.25) | data formatting | bytes 8388608 | tf_op jit(solution)/shard_map/reshape | solution.py:104
  427.5 10.4 %scatter_custom_fusion = f32[64,32768]{1,0:T(8,128)} fusion(s32[32]{0:T(128)S(1)} %reshape.283, f32[32,32768]{1,0:T(8,128)} %bitcast.94, f32[]{:T(128)} %constant.162.clone.1), kind=kCustom, calls=%fused_computation.86 | custom fusion | flops 1048576 | bytes 8389120 | tf_op jit(solution)/shard_map/scatter-add | solution.py:106
  438.0 84.4 %reduce-scatter.2.cloned.1.call-done = f32[16,32768]{1,0:T(8,128)} async-done(((f32[64,32768]{1,0:T(8,128)}), f32[16,32768]{1,0:T(8,128)}) %reduce-scatter.2.cloned.1.call-update) | async-done | bytes 2097168 | tf_op jit(solution)/shard_map/reduce_scatter | solution.py:107
  (69 shorter events, 25.6 us)
Async XLA Ops:
  6.5 92.9 %all-gather.2.cloned.1.call-start = ((), (), s32[]{:S(2)}) async-start(), calls=%async_computation.3 | async-start | bytes 10485760 | tf_op jit(solution)/shard_map/all_gather | solution.py:83
  115.6 4.9 copy-start.3
  115.6 98.8 %all-to-all-start = ((f32[2,2,8,32768]{3,1,0,2:T(2,128)}), f32[2,2,8,32768]{3,1,0,2:T(2,128)}, u32[]{:S(2)}, u32[]{:S(2)}) async-start(f32[2,2,8,32768]{3,1,0,2:T(2,128)} %copy.28), calls=%async_computation | async-start | bytes 8388608 | tf_op jit(solution)/shard_map/all_to_all | solution.py:87
  236.7 1.0 copy-start
  253.0 2.8 copy-start.1
  256.0 1.9 copy-start.2
  268.8 1.0 copy-start
  285.1 2.8 copy-start.1
  288.2 1.9 copy-start.2
  322.4 98.5 %all-to-all-start.1 = ((f32[8,2,2,1,32768]{4,3,2,1,0:T(1,128)}), f32[8,2,2,1,32768]{4,3,2,1,0:T(1,128)}, u32[]{:S(2)}, u32[]{:S(2)}) async-start(f32[8,2,2,1,32768]{4,3,2,1,0:T(1,128)} %fusion.55), calls=%async_computation.1 | async-start | bytes 8388608 | tf_op jit(solution)/shard_map/all_to_all | solution.py:104
  327.0 195.4 %reduce-scatter.2.cloned.1.call-start = ((), (), s32[]{:S(2)}) async-start(), calls=%async_computation.4 | async-start | bytes 10485760 | tf_op jit(solution)/shard_map/reduce_scatter | solution.py:107
Sparse Core Ops, SparseCore 0:
  9.2 90.1 all-gather.1
  438.1 84.2 reduce-scatter.1
